TPU v7x, 256 devices: a whole 4x4x8 slice. The times are simulated.
256 devices in a mesh: traj: 16 (over z, core), amp: 16 (over x, y).
Axes of the slice: x: 4, y: 4, z: 8, core: 2. Of those that a mesh axis runs over, the one named last changes fastest.
Arguments:
- amplitudes: float32 [16, 2, 524288], P('traj', None, 'amp'), parts along dimension 0, may hold values from -6 to 6
- couplings: float32 [18], replicated, may hold values from 0.5 to 2
- fields: float32 [19], replicated, may hold values from 0.5 to 2
- decays: float32 [19], replicated, may hold values from 0.2 to 2
- channel: int32 [16], P('traj'), parts along dimension 0, may hold values from 0 to 19
Outputs:
- evolved_state: float32 [16, 2, 524288], P('traj', None, 'amp'), parts along dimension 0
There are 16 independent parts, one for each index of `traj`. A program takes and returns all parts, laid end to end along the dimension named above; an argument that names none is the same for every part. Nothing has to cross between parts.
Inputs may be any that keep to these rules, and one draw needn't show every extreme that they name: `channel`: the value 19 means that the trajectory does not jump.
All inputs are finite; a program needn't handle non-finite values.
Results may differ from a plain program's by a relative error of at most 0.0003.
Values sent between devices are 32-bit elements; how exact they have to be, the bound alone decides.
A program may use at most 128 MiB of HBM per device.

v0:
```python
import jax
import jax.numpy as jnp
from jax import lax
from jax.sharding import PartitionSpec as P

SPINS = 19
KRYLOV = 8


time_step = 0.7
squarings = 8
taylor_order = 10
highest = lax.Precision.HIGHEST


def copy_for_each(value, axis):
    copies = jnp.broadcast_to(value, (lax.axis_size(axis), *value.shape))
    return lax.all_to_all(copies, axis, split_axis=0, concat_axis=0, tiled=True)


def over_copies(value, axis):
    return copy_for_each(value, axis).sum(axis=0)


def partner_2(value, axis, distance):
    mask = 2**distance
    pairs = [(source, source ^ mask) for source in range(lax.axis_size(axis))]
    return lax.ppermute(value, axis, pairs)


def packed_total(arrays, axis):
    ravelled, at, finished = (jnp.concatenate([a.reshape(-1) for a in arrays]), 0, [])
    running = over_copies(ravelled, axis)
    for a in arrays:
        finished.append(running[at : at + a.size].reshape(a.shape))
        at += a.size
    return tuple(finished)


def flip_axis(tensor, axis_pos, bit_pos):
    old_shape = tensor.shape
    new_shape = (
        old_shape[:axis_pos]
        + (old_shape[axis_pos] >> bit_pos + 1, 2, 1 << bit_pos)
        + old_shape[axis_pos + 1 :]
    )
    return jnp.flip(tensor.reshape(new_shape), axis=axis_pos + 1).reshape(old_shape)


def krylov_weights(scale_norm, hess_real, hess_imag):
    a_real = time_step * hess_imag
    a_imag = -time_step * hess_real
    upper_half = jnp.concatenate([a_real, -a_imag], axis=2)
    lower_half = jnp.concatenate([a_imag, a_real], axis=2)
    scaled = jnp.concatenate([upper_half, lower_half], axis=1) / 2.0**squarings
    identity = jnp.broadcast_to(jnp.eye(2 * KRYLOV, dtype=jnp.float32), scaled.shape)
    series = identity
    for degree in range(taylor_order, 0, -1):
        series = identity + jnp.einsum("tij,tjk->tik", scaled, series, precision=highest) / degree
    for repeat in range(squarings):
        series = jnp.einsum("tij,tjk->tik", series, series, precision=highest)
    first_column = series[:, :, 0] * scale_norm[:, None]
    return (first_column[:, :KRYLOV], first_column[:, KRYLOV:])


def projections(local_proj):
    return over_copies(local_proj, "amp")


def subtract_span(applied, stacked, projected):
    proj_real = projected[:, :, 0]
    proj_imag = projected[:, :, 1]
    comb_real = jnp.einsum(
        "tk,tkrl->trl", proj_real, stacked[:, :, 0], precision=highest
    ) - jnp.einsum("tk,tkrl->trl", proj_imag, stacked[:, :, 1], precision=highest)
    comb_imag = jnp.einsum(
        "tk,tkrl->trl", proj_real, stacked[:, :, 1], precision=highest
    ) + jnp.einsum("tk,tkrl->trl", proj_imag, stacked[:, :, 0], precision=highest)
    return applied - jnp.stack([comb_real, comb_imag], axis=1)


def body(amplitudes, couplings, fields, decays, channel):
    node_count = lax.axis_size("amp")
    high_bits = node_count.bit_length() - 1
    device = lax.axis_index("amp")
    traj_count = amplitudes.shape[0]
    local_len = amplitudes.shape[2]
    row_count = local_len // 128
    block_len = local_len // node_count
    low_spins = SPINS - high_bits
    band_low = SPINS - 2 * high_bits
    local_ids = jnp.arange(local_len, dtype=jnp.int32)
    position = device * local_len + local_ids
    occupation = [(position >> spin_pos & 1).astype(jnp.float32) for spin_pos in range(SPINS)]
    diag_real = jnp.zeros((local_len,), jnp.float32)
    for spin_pos in range(SPINS - 1):
        diag_real = diag_real - couplings[spin_pos] * (1.0 - 2.0 * occupation[spin_pos]) * (
            1.0 - 2.0 * occupation[spin_pos + 1]
        )
    diag_imag = jnp.zeros((local_len,), jnp.float32)
    for spin_pos in range(SPINS):
        diag_imag = diag_imag - 0.5 * decays[spin_pos] * occupation[spin_pos]
    diag_real = diag_real.reshape(row_count, 128)
    diag_imag = diag_imag.reshape(row_count, 128)
    lane_ids = jnp.arange(128, dtype=jnp.int32)
    crossed = lane_ids[:, None] ^ lane_ids[None, :]
    lane_table = jnp.zeros((128, 128), jnp.float32)
    for spin_pos in range(7):
        lane_table = lane_table + fields[spin_pos] * (crossed == 1 << spin_pos).astype(jnp.float32)
    vector = amplitudes.reshape(traj_count, 2, row_count, 128)
    start_sq = over_copies(jnp.sum(vector * vector, axis=(1, 2, 3)), "amp")
    scale_norm = jnp.sqrt(start_sq)
    krylov_basis = [vector / scale_norm[:, None, None, None]]
    hess_real = jnp.zeros((traj_count, KRYLOV, KRYLOV), jnp.float32)
    hess_imag = jnp.zeros((traj_count, KRYLOV, KRYLOV), jnp.float32)
    for column in range(KRYLOV):
        apply_vector = krylov_basis[column]
        flipped = jnp.einsum("tcrl,lm->tcrm", apply_vector, lane_table, precision=highest)
        for apply_spin_pos in range(7, low_spins):
            flipped = flipped + fields[apply_spin_pos] * flip_axis(
                apply_vector, 2, apply_spin_pos - 7
            )
        for apply_bit_pos in range(high_bits):
            partner = partner_2(apply_vector, "amp", apply_bit_pos)
            flipped = flipped + fields[low_spins + apply_bit_pos] * partner
        real_part = apply_vector[:, 0]
        imag_part = apply_vector[:, 1]
        out_real = diag_real * real_part - diag_imag * imag_part - flipped[:, 0]
        out_imag = diag_real * imag_part + diag_imag * real_part - flipped[:, 1]
        applied = jnp.stack([out_real, out_imag], axis=1)
        stacked = jnp.stack(krylov_basis, axis=1)
        swapped = jnp.stack([applied[:, 1], -applied[:, 0]], axis=1)
        paired = jnp.stack([applied, swapped], axis=1)
        local_proj = jnp.einsum("tkcrl,tpcrl->tkp", stacked, paired, precision=highest)
        if column + 1 == KRYLOV:
            projected = projections(local_proj)
        else:
            local_sq = jnp.sum(applied * applied, axis=(1, 2, 3))
            projected, whole_sq = packed_total((local_proj, local_sq), "amp")
            residual = subtract_span(applied, stacked, projected)
            squares = whole_sq - jnp.sum(projected * projected, axis=(1, 2))
            column_norm = jnp.sqrt(squares)
            hess_real = hess_real.at[:, column + 1, column].set(column_norm)
            krylov_basis.append(residual / column_norm[:, None, None, None])
        hess_real = hess_real.at[:, : column + 1, column].set(projected[:, :, 0])
        hess_imag = hess_imag.at[:, : column + 1, column].set(projected[:, :, 1])
    weights_real, weights_imag = krylov_weights(scale_norm, hess_real, hess_imag)
    stacked = jnp.stack(krylov_basis, axis=1)
    new_real = jnp.einsum(
        "tk,tkrl->trl", weights_real, stacked[:, :, 0], precision=highest
    ) - jnp.einsum("tk,tkrl->trl", weights_imag, stacked[:, :, 1], precision=highest)
    new_imag = jnp.einsum(
        "tk,tkrl->trl", weights_real, stacked[:, :, 1], precision=highest
    ) + jnp.einsum("tk,tkrl->trl", weights_imag, stacked[:, :, 0], precision=highest)
    propagated = jnp.stack([new_real, new_imag], axis=1)
    lowered_local = jnp.zeros_like(propagated)
    for spin_pos in range(band_low, low_spins):
        vacant = (local_ids >> spin_pos & 1 == 0).reshape(row_count, 128)
        lowered_term = jnp.where(vacant, flip_axis(propagated, 2, spin_pos - 7), 0.0)
        lowered_local = jnp.where(
            (channel == spin_pos)[:, None, None, None], lowered_term, lowered_local
        )
    spread = propagated.reshape(traj_count, 2, node_count, block_len)
    relaid = lax.all_to_all(spread, "amp", split_axis=2, concat_axis=2, tiled=True)
    sources = jnp.arange(node_count, dtype=jnp.int32)
    offsets = jnp.arange(block_len, dtype=jnp.int32)
    lowered_relaid = jnp.zeros_like(relaid)
    for spin_pos in range(band_low):
        vacant = offsets >> spin_pos & 1 == 0
        lowered_term = jnp.where(vacant, flip_axis(relaid, 3, spin_pos), 0.0)
        lowered_relaid = jnp.where(
            (channel == spin_pos)[:, None, None, None], lowered_term, lowered_relaid
        )
    for bit_pos in range(high_bits):
        vacant = sources >> bit_pos & 1 == 0
        lowered_term = jnp.where(vacant[:, None], flip_axis(relaid, 2, bit_pos), 0.0)
        lowered_relaid = jnp.where(
            (channel == low_spins + bit_pos)[:, None, None, None], lowered_term, lowered_relaid
        )
    returned = lax.all_to_all(
        lowered_relaid, "amp", split_axis=2, concat_axis=2, tiled=True
    ).reshape(propagated.shape)
    in_band = (channel >= band_low) & (channel < low_spins)
    lowered = jnp.where(in_band[:, None, None, None], lowered_local, returned)
    jumped = channel < SPINS
    squared_sum = over_copies(jnp.sum(lowered * lowered, axis=(1, 2, 3)), "amp")
    squared_sum = jnp.where(jumped, squared_sum, jnp.float32(local_len * node_count))
    lowered = lowered * jnp.sqrt(local_len * node_count / squared_sum)[:, None, None, None]
    result = jnp.where(jumped[:, None, None, None], lowered, propagated)
    return result.reshape(traj_count, 2, local_len)


def solution(mesh):
    placed = (P("traj", None, "amp"), P(), P(), P(), P("traj"))
    return jax.shard_map(
        body, mesh=mesh, in_specs=placed, out_specs=P("traj", None, "amp"), check_vma=False
    )
```

profile of v0, /device:TPU:128, one launch (start us, length us, event | category | flops | bytes accessed | tf_op | source)
XLA Modules:
  0.0 840.1 jit_solution(17067351041578492533)
XLA Ops:
  3.1 7.0 all-to-all-start
  59.9 6.9 multiply_add_fusion.7
  66.8 12.0 %slice_subtract_fusion.14 = f32[1,1,256,128]{3,2,1,0:T(8,128)S(1)} fusion(f32[1,2,256,128]{3,2,1,0:T(8,128)S(1)} %multiply_add_fusion.7, f32[1,2,256,128]{3,2,1,0:T(8,128)S(1)} %copy.517, f32[]{:T(128)} %bitcast.23, f32[]{:T(128)} %bitcast.22, f32[]{:T(128)} %bitcast.21, f32[]{:T(128)} %bitcast.20, f32[]{:T(128)} %bitcast.19, f32[]{:T(128)} %bitcast.18, ...), kind=kLoop, calls=%fused_computation.464 | loop fusion | flops 6356992 | bytes 524440 | tf_op jit(solution)/shard_map/sub | solution.py:129
  78.8 12.1 %fusion.366 = (f32[1,1,256,128]{3,2,1,0:T(8,128)S(1)}, f32[1,1,256,128]{3,2,1,0:T(8,128)S(1)}) fusion(f32[1,2,256,128]{3,2,1,0:T(8,128)S(1)} %multiply_add_fusion.7, f32[1,2,256,128]{3,2,1,0:T(8,128)S(1)} %copy.517, f32[]{:T(128)} %bitcast.42, f32[]{:T(128)} %bitcast.41, f32[]{:T(128)} %bitcast.40, f32[]{:T(128)} %bitcast.39, f32[]{:T(128)} %bitcast.38, ...), kind=kLoop, calls=%fused_computation.747 | loop fusion | flops 6389760 | bytes 655512 | tf_op jit(solution)/shard_map/neg | solution.py:132
  99.0 6.5 all-to-all-done.1
  142.6 12.0 %slice_subtract_fusion.12 = f32[1,1,256,128]{3,2,1,0:T(8,128)S(1)} fusion(f32[1,2,256,128]{3,2,1,0:T(8,128)S(1)} %multiply_add_fusion.6, f32[1,2,256,128]{3,2,1,0:T(8,128)S(1)} %fusion.130, f32[]{:T(128)} %bitcast.23, f32[]{:T(128)} %bitcast.22, f32[]{:T(128)} %bitcast.21, f32[]{:T(128)} %bitcast.20, f32[]{:T(128)} %bitcast.19, f32[]{:T(128)} %bitcast.18, ...), kind=kLoop, calls=%fused_computation.462 | loop fusion | flops 6356992 | bytes 524440 | tf_op jit(solution)/shard_map/sub | solution.py:129
  154.6 12.1 %fusion.365 = (f32[1,1,256,128]{3,2,1,0:T(8,128)S(1)}, f32[1,1,256,128]{3,2,1,0:T(8,128)S(1)}) fusion(f32[1,2,256,128]{3,2,1,0:T(8,128)S(1)} %multiply_add_fusion.6, f32[1,2,256,128]{3,2,1,0:T(8,128)S(1)} %fusion.130, f32[]{:T(128)} %bitcast.42, f32[]{:T(128)} %bitcast.41, f32[]{:T(128)} %bitcast.40, f32[]{:T(128)} %bitcast.39, f32[]{:T(128)} %bitcast.38, ...), kind=kLoop, calls=%fused_computation.746 | loop fusion | flops 6389760 | bytes 655512 | tf_op jit(solution)/shard_map/neg | solution.py:132
  232.1 13.0 %slice_subtract_fusion.10 = f32[1,1,256,128]{3,2,1,0:T(8,128)S(1)} fusion(f32[1,2,256,128]{3,2,1,0:T(8,128)S(1)} %multiply_add_fusion.5, f32[1,2,256,128]{3,2,1,0:T(8,128)} %fusion.139, f32[]{:T(128)} %bitcast.23, f32[]{:T(128)} %bitcast.22, f32[]{:T(128)} %bitcast.21, f32[]{:T(128)} %bitcast.20, f32[]{:T(128)} %bitcast.19, f32[]{:T(128)} %bitcast.18, ...), kind=kLoop, calls=%fused_computation.460 | loop fusion | flops 6356992 | bytes 524440 | tf_op jit(solution)/shard_map/sub | solution.py:129
  245.1 13.0 %fusion.364 = (f32[1,1,256,128]{3,2,1,0:T(8,128)S(1)}, f32[1,1,256,128]{3,2,1,0:T(8,128)S(1)}) fusion(f32[1,2,256,128]{3,2,1,0:T(8,128)S(1)} %multiply_add_fusion.5, f32[1,2,256,128]{3,2,1,0:T(8,128)} %fusion.139, f32[]{:T(128)} %bitcast.42, f32[]{:T(128)} %bitcast.41, f32[]{:T(128)} %bitcast.40, f32[]{:T(128)} %bitcast.39, f32[]{:T(128)} %bitcast.38, ...), kind=kLoop, calls=%fused_computation.745 | loop fusion | flops 6389760 | bytes 655512 | tf_op jit(solution)/shard_map/neg | solution.py:132
  332.0 13.0 %slice_subtract_fusion.8 = f32[1,1,256,128]{3,2,1,0:T(8,128)S(1)} fusion(f32[1,2,256,128]{3,2,1,0:T(8,128)S(1)} %multiply_add_fusion.4, f32[1,2,256,128]{3,2,1,0:T(8,128)} %fusion.148, f32[]{:T(128)} %bitcast.23, f32[]{:T(128)} %bitcast.22, f32[]{:T(128)} %bitcast.21, f32[]{:T(128)} %bitcast.20, f32[]{:T(128)} %bitcast.19, f32[]{:T(128)} %bitcast.18, ...), kind=kLoop, calls=%fused_computation.458 | loop fusion | flops 6356992 | bytes 524440 | tf_op jit(solution)/shard_map/sub | solution.py:129
  345.0 13.0 %fusion.363 = (f32[1,1,256,128]{3,2,1,0:T(8,128)S(1)}, f32[1,1,256,128]{3,2,1,0:T(8,128)S(1)}) fusion(f32[1,2,256,128]{3,2,1,0:T(8,128)S(1)} %multiply_add_fusion.4, f32[1,2,256,128]{3,2,1,0:T(8,128)} %fusion.148, f32[]{:T(128)} %bitcast.42, f32[]{:T(128)} %bitcast.41, f32[]{:T(128)} %bitcast.40, f32[]{:T(128)} %bitcast.39, f32[]{:T(128)} %bitcast.38, ...), kind=kLoop, calls=%fused_computation.744 | loop fusion | flops 6389760 | bytes 655512 | tf_op jit(solution)/shard_map/neg | solution.py:132
  424.4 12.0 %slice_subtract_fusion.6 = f32[1,1,256,128]{3,2,1,0:T(8,128)S(1)} fusion(f32[1,2,256,128]{3,2,1,0:T(8,128)S(1)} %multiply_add_fusion.3, f32[1,2,256,128]{3,2,1,0:T(8,128)S(1)} %fusion.157, f32[]{:T(128)} %bitcast.23, f32[]{:T(128)} %bitcast.22, f32[]{:T(128)} %bitcast.21, f32[]{:T(128)} %bitcast.20, f32[]{:T(128)} %bitcast.19, f32[]{:T(128)} %bitcast.18, ...), kind=kLoop, calls=%fused_computation.456 | loop fusion | flops 6356992 | bytes 524440 | tf_op jit(solution)/shard_map/sub | solution.py:129
  436.4 12.2 %fusion.362 = (f32[1,1,256,128]{3,2,1,0:T(8,128)S(1)}, f32[1,1,256,128]{3,2,1,0:T(8,128)S(1)}) fusion(f32[1,2,256,128]{3,2,1,0:T(8,128)S(1)} %multiply_add_fusion.3, f32[1,2,256,128]{3,2,1,0:T(8,128)S(1)} %fusion.157, f32[]{:T(128)} %bitcast.42, f32[]{:T(128)} %bitcast.41, f32[]{:T(128)} %bitcast.40, f32[]{:T(128)} %bitcast.39, f32[]{:T(128)} %bitcast.38, ...), kind=kLoop, calls=%fused_computation.743 | loop fusion | flops 6389760 | bytes 655512 | tf_op jit(solution)/shard_map/neg | solution.py:132
  508.0 12.0 %slice_subtract_fusion.4 = f32[1,1,256,128]{3,2,1,0:T(8,128)S(1)} fusion(f32[1,2,256,128]{3,2,1,0:T(8,128)S(1)} %multiply_add_fusion.2, f32[1,2,256,128]{3,2,1,0:T(8,128)S(1)} %fusion.166, f32[]{:T(128)} %bitcast.23, f32[]{:T(128)} %bitcast.22, f32[]{:T(128)} %bitcast.21, f32[]{:T(128)} %bitcast.20, f32[]{:T(128)} %bitcast.19, f32[]{:T(128)} %bitcast.18, ...), kind=kLoop, calls=%fused_computation.454 | loop fusion | flops 6356992 | bytes 524440 | tf_op jit(solution)/shard_map/sub | solution.py:129
  520.1 12.1 %fusion.361 = (f32[1,1,256,128]{3,2,1,0:T(8,128)S(1)}, f32[1,1,256,128]{3,2,1,0:T(8,128)S(1)}) fusion(f32[1,2,256,128]{3,2,1,0:T(8,128)S(1)} %multiply_add_fusion.2, f32[1,2,256,128]{3,2,1,0:T(8,128)S(1)} %fusion.166, f32[]{:T(128)} %bitcast.42, f32[]{:T(128)} %bitcast.41, f32[]{:T(128)} %bitcast.40, f32[]{:T(128)} %bitcast.39, f32[]{:T(128)} %bitcast.38, ...), kind=kLoop, calls=%fused_computation.742 | loop fusion | flops 6389760 | bytes 655512 | tf_op jit(solution)/shard_map/neg | solution.py:132
  593.7 12.0 %slice_subtract_fusion.2 = f32[1,1,256,128]{3,2,1,0:T(8,128)S(1)} fusion(f32[1,2,256,128]{3,2,1,0:T(8,128)S(1)} %multiply_add_fusion.1, f32[1,2,256,128]{3,2,1,0:T(8,128)S(1)} %fusion.175, f32[]{:T(128)} %bitcast.23, f32[]{:T(128)} %bitcast.22, f32[]{:T(128)} %bitcast.21, f32[]{:T(128)} %bitcast.20, f32[]{:T(128)} %bitcast.19, f32[]{:T(128)} %bitcast.18, ...), kind=kLoop, calls=%fused_computation.452 | loop fusion | flops 6356992 | bytes 524440 | tf_op jit(solution)/shard_map/sub | solution.py:129
  605.8 12.2 %fusion.355 = (f32[1,1,256,128]{3,2,1,0:T(8,128)S(1)}, f32[1,1,256,128]{3,2,1,0:T(8,128)S(1)}) fusion(f32[1,2,256,128]{3,2,1,0:T(8,128)S(1)} %multiply_add_fusion.1, f32[1,2,256,128]{3,2,1,0:T(8,128)S(1)} %fusion.175, f32[]{:T(128)} %bitcast.42, f32[]{:T(128)} %bitcast.41, f32[]{:T(128)} %bitcast.40, f32[]{:T(128)} %bitcast.39, f32[]{:T(128)} %bitcast.38, ...), kind=kLoop, calls=%fused_computation.741 | loop fusion | flops 6389760 | bytes 655512 | tf_op jit(solution)/shard_map/neg | solution.py:132
  678.1 12.0 %slice_subtract_fusion = f32[1,1,256,128]{3,2,1,0:T(8,128)S(1)} fusion(f32[1,2,256,128]{3,2,1,0:T(8,128)S(1)} %multiply_add_fusion, f32[1,2,256,128]{3,2,1,0:T(8,128)S(1)} %fusion.185, f32[]{:T(128)} %bitcast.23, f32[]{:T(128)} %bitcast.22, f32[]{:T(128)} %bitcast.21, f32[]{:T(128)} %bitcast.20, f32[]{:T(128)} %bitcast.19, f32[]{:T(128)} %bitcast.18, ...), kind=kLoop, calls=%fused_computation.450 | loop fusion | flops 6356992 | bytes 524440 | tf_op jit(solution)/shard_map/sub | solution.py:129
  690.2 12.1 %fusion.354 = (f32[1,1,256,128]{3,2,1,0:T(8,128)S(1)}, f32[1,1,256,128]{3,2,1,0:T(8,128)S(1)}) fusion(f32[1,2,256,128]{3,2,1,0:T(8,128)S(1)} %multiply_add_fusion, f32[1,2,256,128]{3,2,1,0:T(8,128)S(1)} %fusion.185, f32[]{:T(128)} %bitcast.42, f32[]{:T(128)} %bitcast.41, f32[]{:T(128)} %bitcast.40, f32[]{:T(128)} %bitcast.39, f32[]{:T(128)} %bitcast.38, ...), kind=kLoop, calls=%fused_computation.740 | loop fusion | flops 6389760 | bytes 655512 | tf_op jit(solution)/shard_map/neg | solution.py:132
  741.0 7.7 all-to-all-done.9
  751.6 7.9 rev.354
  779.8 9.6 %rev.350 = f32[1,2,16,64,2,16]{5,4,3,2,1,0:T(2,128)S(1)} reverse(f32[1,2,16,64,2,16]{5,4,3,2,1,0:T(2,128)} %reshape.8040), dimensions={4} | reverse | bytes 524288 | tf_op jit(solution)/shard_map/jit(_flip)/rev | solution.py:47
  816.1 7.5 all-to-all-done.10
  829.5 7.3 all-to-all-done.11
  (664 shorter events, 557.0 us)
Async XLA Ops:
  3.1 37.2 %all-to-all-start = ((f32[16,1,1]{2,1,0:T(1,128)}), f32[16,1,1]{2,1,0:T(1,128)S(1)}, u32[]{:S(2)}, u32[]{:S(2)}) async-start(f32[16,1,1]{2,1,0:T(1,128)} %broadcast_in_dim.346), calls=%async_computation | async-start | bytes 16384 | tf_op jit(solution)/shard_map/all_to_all | solution.py:18
  110.2 28.7 %collective-permute-start.7 = (f32[1,2,256,128]{3,2,1,0:T(8,128)S(1)}, f32[1,2,256,128]{3,2,1,0:T(8,128)}, u32[]{:S(2)}, u32[]{:S(2)}) collective-permute-start(f32[1,2,256,128]{3,2,1,0:T(8,128)S(1)} %fusion.130), channel_id=1, source_target_pairs={{0,8},{1,9},{2,10},{3,11},{4,12},{5,13},{6,14},{7,15},{8,0},{9,1},... | collective-permute-start | bytes 786440 | tf_op jit(solution)/shard_map/ppermute | solution.py:28
  111.4 27.5 %collective-permute-start.6 = (f32[1,2,256,128]{3,2,1,0:T(8,128)S(1)}, f32[1,2,256,128]{3,2,1,0:T(8,128)}, u32[]{:S(2)}, u32[]{:S(2)}) collective-permute-start(f32[1,2,256,128]{3,2,1,0:T(8,128)S(1)} %fusion.130), channel_id=1, source_target_pairs={{0,4},{1,5},{2,6},{3,7},{4,0},{5,1},{6,2},{7,3},{8,12},{9,13},{10,... | collective-permute-start | bytes 786440 | tf_op jit(solution)/shard_map/ppermute | solution.py:28
  112.3 26.6 %collective-permute-start.5 = (f32[1,2,256,128]{3,2,1,0:T(8,128)S(1)}, f32[1,2,256,128]{3,2,1,0:T(8,128)}, u32[]{:S(2)}, u32[]{:S(2)}) collective-permute-start(f32[1,2,256,128]{3,2,1,0:T(8,128)S(1)} %fusion.130), channel_id=1, source_target_pairs={{0,2},{1,3},{2,0},{3,1},{4,6},{5,7},{6,4},{7,5},{8,10},{9,11},{10,... | collective-permute-start | bytes 786440 | tf_op jit(solution)/shard_map/ppermute | solution.py:28
  113.5 25.4 %collective-permute-start.4 = (f32[1,2,256,128]{3,2,1,0:T(8,128)S(1)}, f32[1,2,256,128]{3,2,1,0:T(8,128)}, u32[]{:S(2)}, u32[]{:S(2)}) collective-permute-start(f32[1,2,256,128]{3,2,1,0:T(8,128)S(1)} %fusion.130), channel_id=1, source_target_pairs={{0,1},{1,0},{2,3},{3,2},{4,5},{5,4},{6,7},{7,6},{8,9},{9,8},{10,11... | collective-permute-start | bytes 786440 | tf_op jit(solution)/shard_map/ppermute | solution.py:28
  198.3 30.2 %collective-permute-start.11 = (f32[1,2,256,128]{3,2,1,0:T(8,128)}, f32[1,2,256,128]{3,2,1,0:T(8,128)}, u32[]{:S(2)}, u32[]{:S(2)}) collective-permute-start(f32[1,2,256,128]{3,2,1,0:T(8,128)} %fusion.139), channel_id=1, source_target_pairs={{0,8},{1,9},{2,10},{3,11},{4,12},{5,13},{6,14},{7,15},{8,0},{9,1},... | collective-permute-start | bytes 786440 | tf_op jit(solution)/shard_map/ppermute | solution.py:28
  199.4 29.0 %collective-permute-start.10 = (f32[1,2,256,128]{3,2,1,0:T(8,128)}, f32[1,2,256,128]{3,2,1,0:T(8,128)}, u32[]{:S(2)}, u32[]{:S(2)}) collective-permute-start(f32[1,2,256,128]{3,2,1,0:T(8,128)} %fusion.139), channel_id=1, source_target_pairs={{0,4},{1,5},{2,6},{3,7},{4,0},{5,1},{6,2},{7,3},{8,12},{9,13},{10,... | collective-permute-start | bytes 786440 | tf_op jit(solution)/shard_map/ppermute | solution.py:28
  200.3 28.2 %collective-permute-start.9 = (f32[1,2,256,128]{3,2,1,0:T(8,128)}, f32[1,2,256,128]{3,2,1,0:T(8,128)}, u32[]{:S(2)}, u32[]{:S(2)}) collective-permute-start(f32[1,2,256,128]{3,2,1,0:T(8,128)} %fusion.139), channel_id=1, source_target_pairs={{0,2},{1,3},{2,0},{3,1},{4,6},{5,7},{6,4},{7,5},{8,10},{9,11},{10,... | collective-permute-start | bytes 786440 | tf_op jit(solution)/shard_map/ppermute | solution.py:28
  201.5 27.0 %collective-permute-start.8 = (f32[1,2,256,128]{3,2,1,0:T(8,128)}, f32[1,2,256,128]{3,2,1,0:T(8,128)}, u32[]{:S(2)}, u32[]{:S(2)}) collective-permute-start(f32[1,2,256,128]{3,2,1,0:T(8,128)} %fusion.139), channel_id=1, source_target_pairs={{0,1},{1,0},{2,3},{3,2},{4,5},{5,4},{6,7},{7,6},{8,9},{9,8},{10,11... | collective-permute-start | bytes 786440 | tf_op jit(solution)/shard_map/ppermute | solution.py:28
  297.6 30.7 %collective-permute-start.15 = (f32[1,2,256,128]{3,2,1,0:T(8,128)}, f32[1,2,256,128]{3,2,1,0:T(8,128)}, u32[]{:S(2)}, u32[]{:S(2)}) collective-permute-start(f32[1,2,256,128]{3,2,1,0:T(8,128)} %fusion.148), channel_id=1, source_target_pairs={{0,8},{1,9},{2,10},{3,11},{4,12},{5,13},{6,14},{7,15},{8,0},{9,1},... | collective-permute-start | bytes 786440 | tf_op jit(solution)/shard_map/ppermute | solution.py:28
  299.1 29.2 %collective-permute-start.14 = (f32[1,2,256,128]{3,2,1,0:T(8,128)}, f32[1,2,256,128]{3,2,1,0:T(8,128)}, u32[]{:S(2)}, u32[]{:S(2)}) collective-permute-start(f32[1,2,256,128]{3,2,1,0:T(8,128)} %fusion.148), channel_id=1, source_target_pairs={{0,4},{1,5},{2,6},{3,7},{4,0},{5,1},{6,2},{7,3},{8,12},{9,13},{10,... | collective-permute-start | bytes 786440 | tf_op jit(solution)/shard_map/ppermute | solution.py:28
  299.9 28.4 %collective-permute-start.13 = (f32[1,2,256,128]{3,2,1,0:T(8,128)}, f32[1,2,256,128]{3,2,1,0:T(8,128)}, u32[]{:S(2)}, u32[]{:S(2)}) collective-permute-start(f32[1,2,256,128]{3,2,1,0:T(8,128)} %fusion.148), channel_id=1, source_target_pairs={{0,2},{1,3},{2,0},{3,1},{4,6},{5,7},{6,4},{7,5},{8,10},{9,11},{10,... | collective-permute-start | bytes 786440 | tf_op jit(solution)/shard_map/ppermute | solution.py:28
  301.6 26.7 %collective-permute-start.12 = (f32[1,2,256,128]{3,2,1,0:T(8,128)}, f32[1,2,256,128]{3,2,1,0:T(8,128)}, u32[]{:S(2)}, u32[]{:S(2)}) collective-permute-start(f32[1,2,256,128]{3,2,1,0:T(8,128)} %fusion.148), channel_id=1, source_target_pairs={{0,1},{1,0},{2,3},{3,2},{4,5},{5,4},{6,7},{7,6},{8,9},{9,8},{10,11... | collective-permute-start | bytes 786440 | tf_op jit(solution)/shard_map/ppermute | solution.py:28
  393.1 27.6 %collective-permute-start.19 = (f32[1,2,256,128]{3,2,1,0:T(8,128)S(1)}, f32[1,2,256,128]{3,2,1,0:T(8,128)}, u32[]{:S(2)}, u32[]{:S(2)}) collective-permute-start(f32[1,2,256,128]{3,2,1,0:T(8,128)S(1)} %fusion.157), channel_id=1, source_target_pairs={{0,8},{1,9},{2,10},{3,11},{4,12},{5,13},{6,14},{7,15},{8,0},{9,1},... | collective-permute-start | bytes 786440 | tf_op jit(solution)/shard_map/ppermute | solution.py:28
  394.4 26.4 %collective-permute-start.18 = (f32[1,2,256,128]{3,2,1,0:T(8,128)S(1)}, f32[1,2,256,128]{3,2,1,0:T(8,128)}, u32[]{:S(2)}, u32[]{:S(2)}) collective-permute-start(f32[1,2,256,128]{3,2,1,0:T(8,128)S(1)} %fusion.157), channel_id=1, source_target_pairs={{0,4},{1,5},{2,6},{3,7},{4,0},{5,1},{6,2},{7,3},{8,12},{9,13},{10,... | collective-permute-start | bytes 786440 | tf_op jit(solution)/shard_map/ppermute | solution.py:28
  395.2 25.5 %collective-permute-start.17 = (f32[1,2,256,128]{3,2,1,0:T(8,128)S(1)}, f32[1,2,256,128]{3,2,1,0:T(8,128)}, u32[]{:S(2)}, u32[]{:S(2)}) collective-permute-start(f32[1,2,256,128]{3,2,1,0:T(8,128)S(1)} %fusion.157), channel_id=1, source_target_pairs={{0,2},{1,3},{2,0},{3,1},{4,6},{5,7},{6,4},{7,5},{8,10},{9,11},{10,... | collective-permute-start | bytes 786440 | tf_op jit(solution)/shard_map/ppermute | solution.py:28
  397.4 23.3 %collective-permute-start.16 = (f32[1,2,256,128]{3,2,1,0:T(8,128)S(1)}, f32[1,2,256,128]{3,2,1,0:T(8,128)}, u32[]{:S(2)}, u32[]{:S(2)}) collective-permute-start(f32[1,2,256,128]{3,2,1,0:T(8,128)S(1)} %fusion.157), channel_id=1, source_target_pairs={{0,1},{1,0},{2,3},{3,2},{4,5},{5,4},{6,7},{7,6},{8,9},{9,8},{10,11... | collective-permute-start | bytes 786440 | tf_op jit(solution)/shard_map/ppermute | solution.py:28
  479.2 25.2 %collective-permute-start.23 = (f32[1,2,256,128]{3,2,1,0:T(8,128)S(1)}, f32[1,2,256,128]{3,2,1,0:T(8,128)}, u32[]{:S(2)}, u32[]{:S(2)}) collective-permute-start(f32[1,2,256,128]{3,2,1,0:T(8,128)S(1)} %fusion.166), channel_id=1, source_target_pairs={{0,8},{1,9},{2,10},{3,11},{4,12},{5,13},{6,14},{7,15},{8,0},{9,1},... | collective-permute-start | bytes 786440 | tf_op jit(solution)/shard_map/ppermute | solution.py:28
  480.4 24.0 %collective-permute-start.22 = (f32[1,2,256,128]{3,2,1,0:T(8,128)S(1)}, f32[1,2,256,128]{3,2,1,0:T(8,128)}, u32[]{:S(2)}, u32[]{:S(2)}) collective-permute-start(f32[1,2,256,128]{3,2,1,0:T(8,128)S(1)} %fusion.166), channel_id=1, source_target_pairs={{0,4},{1,5},{2,6},{3,7},{4,0},{5,1},{6,2},{7,3},{8,12},{9,13},{10,... | collective-permute-start | bytes 786440 | tf_op jit(solution)/shard_map/ppermute | solution.py:28
  481.3 23.1 %collective-permute-start.21 = (f32[1,2,256,128]{3,2,1,0:T(8,128)S(1)}, f32[1,2,256,128]{3,2,1,0:T(8,128)}, u32[]{:S(2)}, u32[]{:S(2)}) collective-permute-start(f32[1,2,256,128]{3,2,1,0:T(8,128)S(1)} %fusion.166), channel_id=1, source_target_pairs={{0,2},{1,3},{2,0},{3,1},{4,6},{5,7},{6,4},{7,5},{8,10},{9,11},{10,... | collective-permute-start | bytes 786440 | tf_op jit(solution)/shard_map/ppermute | solution.py:28
  565.2 24.8 %collective-permute-start.27 = (f32[1,2,256,128]{3,2,1,0:T(8,128)S(1)}, f32[1,2,256,128]{3,2,1,0:T(8,128)}, u32[]{:S(2)}, u32[]{:S(2)}) collective-permute-start(f32[1,2,256,128]{3,2,1,0:T(8,128)S(1)} %fusion.175), channel_id=1, source_target_pairs={{0,8},{1,9},{2,10},{3,11},{4,12},{5,13},{6,14},{7,15},{8,0},{9,1},... | collective-permute-start | bytes 786440 | tf_op jit(solution)/shard_map/ppermute | solution.py:28
  566.5 23.6 %collective-permute-start.26 = (f32[1,2,256,128]{3,2,1,0:T(8,128)S(1)}, f32[1,2,256,128]{3,2,1,0:T(8,128)}, u32[]{:S(2)}, u32[]{:S(2)}) collective-permute-start(f32[1,2,256,128]{3,2,1,0:T(8,128)S(1)} %fusion.175), channel_id=1, source_target_pairs={{0,4},{1,5},{2,6},{3,7},{4,0},{5,1},{6,2},{7,3},{8,12},{9,13},{10,... | collective-permute-start | bytes 786440 | tf_op jit(solution)/shard_map/ppermute | solution.py:28
  649.4 25.1 %collective-permute-start.31 = (f32[1,2,256,128]{3,2,1,0:T(8,128)S(1)}, f32[1,2,256,128]{3,2,1,0:T(8,128)}, u32[]{:S(2)}, u32[]{:S(2)}) collective-permute-start(f32[1,2,256,128]{3,2,1,0:T(8,128)S(1)} %fusion.185), channel_id=1, source_target_pairs={{0,8},{1,9},{2,10},{3,11},{4,12},{5,13},{6,14},{7,15},{8,0},{9,1},... | collective-permute-start | bytes 786440 | tf_op jit(solution)/shard_map/ppermute | solution.py:28
  650.7 23.8 %collective-permute-start.30 = (f32[1,2,256,128]{3,2,1,0:T(8,128)S(1)}, f32[1,2,256,128]{3,2,1,0:T(8,128)}, u32[]{:S(2)}, u32[]{:S(2)}) collective-permute-start(f32[1,2,256,128]{3,2,1,0:T(8,128)S(1)} %fusion.185), channel_id=1, source_target_pairs={{0,4},{1,5},{2,6},{3,7},{4,0},{5,1},{6,2},{7,3},{8,12},{9,13},{10,... | collective-permute-start | bytes 786440 | tf_op jit(solution)/shard_map/ppermute | solution.py:28
  (80 other events, 863.4 us)
where the time goes:
time: 855 us; the launch traced here: 840 us
  other arithmetic  366 us (43%)
  local copies, waits for them, and re-layouts  155 us (18%)
  matrix products  130 us (15%)
  starting transfers between devices  105 us (12%)
  waiting for transfers between devices  58.4 us (7%)
  between operations  25.7 us (3%)
    neg x8, other arithmetic, body(): swapped = jnp.stack([applied[:, 1], -applied[:, 0]], axis=1)  98.7 us
    sub x8, other arithmetic, body(): out_imag = diag_real * imag_part + diag_imag * real_part - flipped[:, 1]  98.2 us
    mul x64, other arithmetic, body(): fields[apply_spin_pos] * flip_axis(apply_vector, 2, apply_spin_pos - 7)  81.5 us
    all_to_all x10, starting transfers between devices, copy_for_each(): return lax.all_to_all(copies, axis, split_axis=0, concat_axis=0, tiled=True)  56.6 us
    dot_general x8, matrix products, body(): jnp.einsum('tcrl,lm->tcrm', apply_vector, lane_table, precision=highest)  47.3 us
    another operation x35, local copies, waits for them, and re-layouts  42.6 us
    ppermute x32, starting transfers between devices, partner_2(): return lax.ppermute(value, axis, pairs)  39.8 us
    dot_general x7, matrix products, body(): jnp.einsum('tkcrl,tpcrl->tkp', stacked, paired, precision=highest)  39.1 us
  transfers between devices with their start and end apart: 44, of which 13 were waited for; matrix products, arithmetic and copies ran while one was open for 25% of the time, Pallas kernels for 0%

commit v1 on v0

v1 whole, which is shorter than its diff:
```python
import functools

import jax
import jax.numpy as jnp
from jax import lax
from jax.experimental import pallas as pl
from jax.experimental.pallas import tpu as pltpu
from jax.sharding import PartitionSpec as P

SPINS = 19
KRYLOV = 8
TILES = 32
CHUNKS = 8
PER = TILES // CHUNKS
CHUNK_BITS = CHUNKS.bit_length() - 1
EARLY = 2
TIME_STEP = 0.7
MESH = pl.DeviceIdType.MESH
OWN, DIR_Y, DIR_X, REL_Y, REL_X = range(5)
highest = lax.Precision.HIGHEST
f32 = jnp.float32


def flip(index, bit):
    step = 1 << bit
    return index + step - 2 * step * ((index // step) % 2)


def flip_by(index, mask):
    for bit in range(4):
        if mask >> bit & 1:
            index = flip(index, bit)
    return index


def wide(value):
    return jnp.broadcast_to(value, (8, 128))


def cmul(ar, ai, br, bi):
    return ar * br - ai * bi, ar * bi + ai * br


def matmul8(ar, ai, br, bi):
    out_r, out_i = None, None
    for k in range(KRYLOV):
        cr, ci = ar[:, k : k + 1], ai[:, k : k + 1]
        rr, ri = br[k : k + 1, :], bi[k : k + 1, :]
        tr, ti = cr * rr - ci * ri, cr * ri + ci * rr
        out_r = tr if out_r is None else out_r + tr
        out_i = ti if out_i is None else out_i + ti
    return out_r, out_i


def kernel(
    amp_ref, coup, field, decay, chan, out_ref,
    big, vbuf, zbuf, hbuf, diag_r, diag_i, mask_ref, lanes_ref, acc, total_ref, gather, prop,
    recv_sem, send_sem, red_recv, red_send,
):
    me = lax.axis_index("amp")
    y, x = me % 4, me // 4
    near_y, near_x = x * 4 + flip(y, 0), flip(x, 0) * 4 + y
    far_y, far_x = x * 4 + 3 - y, (3 - x) * 4 + y

    barrier = pltpu.get_barrier_semaphore()
    for mask in range(1, 16):
        pl.semaphore_signal(barrier, inc=1, device_id={"amp": flip_by(me, mask)}, device_id_type=MESH)

    lane = lax.broadcasted_iota(jnp.int32, (8, 128), 1)
    sub = lax.broadcasted_iota(jnp.int32, (8, 128), 0)
    low = sub * 128 + lane

    def direct(step, chunk):
        made = []
        for kind, target in ((DIR_Y, near_y), (DIR_X, near_x)):
            made.append(pltpu.make_async_remote_copy(
                src_ref=big.at[OWN, step, chunk], dst_ref=big.at[kind, step, chunk],
                send_sem=send_sem.at[kind - 1, step], recv_sem=recv_sem.at[kind - 1, step, chunk],
                device_id={"amp": target}, device_id_type=MESH))
        return made

    def relay(step, chunk):
        made = []
        for kind, source, target in ((REL_Y, DIR_Y, far_y), (REL_X, DIR_X, far_x)):
            made.append(pltpu.make_async_remote_copy(
                src_ref=big.at[source, step, chunk], dst_ref=big.at[kind, step, chunk],
                send_sem=send_sem.at[kind - 1, step], recv_sem=recv_sem.at[kind - 1, step, chunk],
                device_id={"amp": target}, device_id_type=MESH))
        return made

    def sum_copy(number, mask):
        return pltpu.make_async_remote_copy(
            src_ref=total_ref.at[number], dst_ref=gather.at[number, mask - 1],
            send_sem=red_send.at[number], recv_sem=red_recv.at[number],
            device_id={"amp": flip_by(me, mask)}, device_id_type=MESH)

    def post_sums(number):
        rows = lax.broadcasted_iota(jnp.int32, (40, 128), 0)
        cols = lax.broadcasted_iota(jnp.int32, (40, 128), 1)
        by_lane = jnp.sum(acc[...], axis=1)
        by_row = jnp.sum(by_lane, axis=1, keepdims=True)
        total_ref[number] = jnp.sum(jnp.where(rows == cols, by_row, 0.0), axis=0, keepdims=True)
        for mask in range(1, 16):
            sum_copy(number, mask).start()

    def take_sums(number):
        pltpu.make_async_copy(gather.at[number], gather.at[number], red_recv.at[number]).wait()
        terms = [total_ref[number]] + [gather[number, i] for i in range(15)]
        while len(terms) > 1:
            terms = [terms[i] + terms[i + 1] for i in range(0, len(terms), 2)]
        return wide(terms[0])

    def pick(row, at):
        return wide(jnp.sum(jnp.where(lane == at, row, 0.0), axis=1, keepdims=True))

    z = [1.0 - 2.0 * (low >> i & 1).astype(f32) for i in range(10)]
    base_r = jnp.zeros((8, 128), f32)
    base_i = jnp.zeros((8, 128), f32)
    for i in range(9):
        base_r = base_r - coup[i] * (z[i] * z[i + 1])
    for i in range(10):
        base_i = base_i - (0.25 * decay[i]) * (1.0 - z[i])
    zdev = [(1 - 2 * ((me // (1 << b)) % 2)).astype(f32) for b in range(4)]
    dev_r = -(coup[15] * zdev[0] * zdev[1] + coup[16] * zdev[1] * zdev[2] + coup[17] * zdev[2] * zdev[3])
    dev_i = jnp.float32(0.0)
    for b in range(4):
        dev_i = dev_i - 0.25 * decay[15 + b] * (1.0 - zdev[b])
    bond = coup[9] * z[9]
    channel = chan[0]
    for tile in range(TILES):
        zt = [1.0 - 2.0 * (tile >> b & 1) for b in range(5)]
        sr, si = dev_r - coup[14] * zdev[0] * zt[4], dev_i
        for b in range(4):
            sr = sr - coup[10 + b] * (zt[b] * zt[b + 1])
        for b in range(5):
            if tile >> b & 1:
                si = si - 0.5 * decay[10 + b]
        diag_r[tile // PER, tile % PER] = (base_r - bond * zt[0]) + sr
        diag_i[tile // PER, tile % PER] = base_i + si
        spot = low + (tile * 1024 + me * 32768)
        mask_ref[tile // PER, tile % PER] = (spot >> jnp.full((8, 128), channel, jnp.int32) & 1).astype(f32)
    li = lax.broadcasted_iota(jnp.int32, (128, 128), 0)
    lj = lax.broadcasted_iota(jnp.int32, (128, 128), 1)
    table = jnp.zeros((128, 128), f32)
    for i in range(7):
        table = table + jnp.where((li ^ lj) == 1 << i, field[i], 0.0)
    lanes_ref[...] = table
    for part in range(2):
        for chunk in range(CHUNKS):
            big[OWN, 0, chunk, part] = amp_ref[part, chunk * PER : (chunk + 1) * PER]
    acc[...] = jnp.zeros((40, 8, 128), f32)

    def local_part(step, chunk):
        v = big[OWN, step, chunk]
        flips = lax.dot_general(
            v.reshape(2 * PER * 8, 128), lanes_ref[...], (((1,), (0,)), ((), ())),
            precision=highest, preferred_element_type=f32).reshape(2 * PER, 8, 128)
        w = v.reshape(2 * PER, 8, 128)
        s3 = lax.broadcasted_iota(jnp.int32, (2 * PER, 8, 128), 1)
        for b in range(2):
            step_rows = 1 << b
            up = pltpu.roll(w, 8 - step_rows, 1)
            down = pltpu.roll(w, step_rows, 1)
            flips = flips + field[7 + b] * jnp.where((s3 >> b & 1) == 0, up, down)
        flips = flips + field[9] * pltpu.roll(w, 4, 1)
        flips = flips.reshape(2, PER, 8, 128)
        for b in range(5 - CHUNK_BITS):
            order = [t ^ (1 << b) for t in range(PER)]
            flips = flips + field[10 + b] * jnp.concatenate([v[:, t : t + 1] for t in order], axis=1)
        for b in range(CHUNK_BITS):
            flips = flips + field[15 - CHUNK_BITS + b] * big[OWN, step, flip(chunk, b)]
        dr, di = diag_r[chunk], diag_i[chunk]
        hr = dr * v[0] - di * v[1] - flips[0]
        hi = dr * v[1] + di * v[0] - flips[1]
        return v, hr, hi

    pl.semaphore_wait(barrier, 15)

    def send_first(chunk, carry):
        for copy in direct(0, chunk):
            copy.start()
        return carry

    lax.fori_loop(0, CHUNKS, send_first, 0)

    def first(chunk, carry):
        v, hr, hi = local_part(0, chunk)
        hbuf[chunk, 0] = hr
        hbuf[chunk, 1] = hi
        acc[0] += jnp.sum(v[0] * hr + v[1] * hi, axis=0)
        acc[8] += jnp.sum(v[0] * hi - v[1] * hr, axis=0)
        acc[32] += jnp.sum(v[0] * v[0] + v[1] * v[1], axis=0)
        return carry

    lax.fori_loop(0, CHUNKS, first, 0)
    post_sums(0)

    zero = jnp.zeros((8, 128), f32)
    hess_r, hess_i = zero, zero
    basis_r, basis_i = zero, zero
    proj_r, proj_i = zero, zero
    shift_r, shift_i, back = zero, zero, zero
    beta = zero

    def imag_of(row):
        return pltpu.roll(row, 128 - 8, 1)

    for step in range(KRYLOV + 1):
        if step < KRYLOV:
            if step > 0:
                def local(chunk, carry, step=step):
                    _, hr, hi = local_part(step, chunk)
                    hbuf[chunk, 0] = hr
                    hbuf[chunk, 1] = hi
                    return carry

                lax.fori_loop(0, CHUNKS, local, 0)

            def forward(chunk, carry, step=step):
                for copy in direct(step, chunk):
                    copy.wait_recv()
                for copy in relay(step, chunk):
                    copy.start()
                hbuf[chunk] = hbuf[chunk] - (
                    field[15] * big[DIR_Y, step, chunk] + field[17] * big[DIR_X, step, chunk])
                return carry

            lax.fori_loop(0, CHUNKS, forward, 0)
        row = take_sums(step)
        row_i = imag_of(row)
        square = pick(row, 32)
        if step == 0:
            norm = jnp.sqrt(square)
            shift_r = pick(row, 0) / square
            shift_i = pick(row, 8) / square
            beta = norm
            gs = []
        else:
            gs = [(pick(row, k), pick(row, 8 + k)) for k in range(step)]
            used = square
            for gr, gi in gs:
                used = used - (gr * gr + gi * gi)
            norm = jnp.sqrt(used)
            at = sub == step - 1
            col_r = jnp.where(lane < step, row, 0.0) + jnp.where(lane == step - 1, shift_r, 0.0)
            col_i = jnp.where(lane < step, row_i, 0.0) + jnp.where(lane == step - 1, shift_i, 0.0)
            if step > 1:
                col_r = col_r + jnp.where(lane == step - 2, back, 0.0)
            if step < KRYLOV:
                col_r = col_r + jnp.where(lane == step, norm, 0.0)
            hess_r = jnp.where(at, col_r, hess_r)
            hess_i = jnp.where(at, col_i, hess_i)
            pr = pltpu.roll(row, 128 - 16, 1)
            proj_r = jnp.where(at & (lane < step), pr, proj_r)
            proj_i = jnp.where(at & (lane < step), imag_of(pr), proj_i)
            shift_r = shift_r + gs[-1][0]
            shift_i = shift_i + gs[-1][1]
            back = norm
        if step == KRYLOV:
            break
        inv = 1.0 / norm
        br, bi = jnp.where(lane[:1] == step, 1.0, 0.0), jnp.zeros((1, 128), f32)
        for k, (gr, gi) in enumerate(gs):
            tr, ti = cmul(gr[:1], gi[:1], basis_r[k : k + 1], basis_i[k : k + 1])
            br, bi = br - tr, bi - ti
        basis_r = jnp.where(sub == step, wide(br * inv[:1]), basis_r)
        basis_i = jnp.where(sub == step, wide(bi * inv[:1]), basis_i)

        acc[...] = jnp.zeros((40, 8, 128), f32)

        def advance(chunk, carry, step=step, gs=gs, inv=inv, shift_r=shift_r, shift_i=shift_i, back=back):
            for copy in relay(step, chunk):
                copy.wait_recv()
            h = hbuf[chunk] - (field[16] * big[REL_Y, step, chunk] + field[18] * big[REL_X, step, chunk])
            v = big[OWN, step, chunk]
            vr, vi, zr, zi = v[0], v[1], h[0], h[1]
            for k, (gr, gi) in enumerate(gs):
                pv, pz = vbuf[k, chunk], zbuf[k, chunk]
                tr, ti = cmul(gr, gi, pv[0], pv[1])
                vr, vi = vr - tr, vi - ti
                tr, ti = cmul(gr, gi, pz[0], pz[1])
                zr, zi = zr - tr, zi - ti
            vr, vi, zr, zi = vr * inv, vi * inv, zr * inv, zi * inv
            tr, ti = cmul(shift_r, shift_i, vr, vi)
            ur, ui = zr - tr, zi - ti
            if step > 0:
                pv = vbuf[step - 1, chunk]
                ur, ui = ur - back * pv[0], ui - back * pv[1]
            if step + 1 < KRYLOV:
                vbuf[step, chunk, 0] = vr
                vbuf[step, chunk, 1] = vi
                zbuf[step, chunk, 0] = zr
                zbuf[step, chunk, 1] = zi
                big[OWN, step + 1, chunk, 0] = ur
                big[OWN, step + 1, chunk, 1] = ui
            m = mask_ref[chunk]
            mr, mi = m * vr, m * vi
            for k in range(step + 1):
                if k < step:
                    pv = vbuf[k, chunk]
                    pr, pi = pv[0], pv[1]
                else:
                    pr, pi = vr, vi
                acc[k] += jnp.sum(pr * ur + pi * ui, axis=0)
                acc[8 + k] += jnp.sum(pr * ui - pi * ur, axis=0)
                acc[16 + k] += jnp.sum(pr * mr + pi * mi, axis=0)
                acc[24 + k] += jnp.sum(pr * mi - pi * mr, axis=0)
            acc[32] += jnp.sum(ur * ur + ui * ui, axis=0)
            if step + 1 < KRYLOV:
                @pl.when((chunk >= 1) & (chunk <= EARLY))
                def _():
                    for copy in direct(step + 1, chunk - 1):
                        copy.start()
            return carry

        lax.fori_loop(0, CHUNKS, advance, 0)
        post_sums(step + 1)
        if step + 1 < KRYLOV:
            def send_rest(chunk, carry, step=step):
                for copy in direct(step + 1, chunk):
                    copy.start()
                return carry

            lax.fori_loop(EARLY, CHUNKS, send_rest, 0)

    scale = TIME_STEP / 256.0
    ar, ai = scale * hess_i, -scale * hess_r
    eye = jnp.where(sub == lane, 1.0, 0.0)
    er, ei = eye, zero
    for degree in range(10, 0, -1):
        tr, ti = matmul8(ar, ai, er, ei)
        er, ei = eye + tr * (1.0 / degree), ti * (1.0 / degree)
    for _ in range(8):
        er, ei = matmul8(er, ei, er, ei)
    first_r, first_i = wide(er[:1]) * beta, wide(ei[:1]) * beta
    along_r = wide(jnp.sum(jnp.where(sub == lane, first_r, 0.0), axis=1, keepdims=True))
    along_i = wide(jnp.sum(jnp.where(sub == lane, first_i, 0.0), axis=1, keepdims=True))
    pair_r, pair_i = cmul(first_r, -first_i, along_r, along_i)
    weight = jnp.where(lane < sub, 2.0, 1.0)
    weighed = jnp.where(lane < KRYLOV, weight * (pair_r * proj_r - pair_i * proj_i), 0.0)
    held = wide(jnp.sum(jnp.sum(weighed, axis=1, keepdims=True), axis=0, keepdims=True))
    jumps = jnp.full((8, 128), channel, jnp.int32)
    held = jnp.where(jumps < SPINS, held, 524288.0)
    factor = jnp.sqrt(524288.0 / held)
    tr, ti = cmul(along_r, along_i, basis_r, basis_i)
    sent_r = wide(jnp.sum(tr, axis=0, keepdims=True)) * factor
    sent_i = wide(jnp.sum(ti, axis=0, keepdims=True)) * factor
    ds = [(pick(sent_r, k), pick(sent_i, k)) for k in range(KRYLOV)]

    source = jnp.where(channel == 15, DIR_Y, OWN)
    source = jnp.where(channel == 17, DIR_X, source)
    source = jnp.where(channel == 16, REL_Y, source)
    source = jnp.where(channel == 18, REL_X, source)

    def combine(chunk, carry):
        tot_r, tot_i = None, None
        for k, (dr, di) in enumerate(ds):
            v = big[source, k, chunk]
            tr, ti = cmul(dr, di, v[0], v[1])
            tot_r = tr if tot_r is None else tot_r + tr
            tot_i = ti if tot_i is None else tot_i + ti
        prop[0, chunk] = tot_r
        prop[1, chunk] = tot_i
        return carry

    lax.fori_loop(0, CHUNKS, combine, 0)
    delta = jnp.where((channel >= 10) & (channel < 15), jnp.left_shift(1, jnp.clip(channel - 10, 0, 4)), 0)

    def jump(chunk, carry):
        for t in range(PER):
            at = jnp.minimum(chunk * PER + t + delta, TILES - 1)
            vacant = 1.0 - mask_ref[chunk, t]
            for part in range(2):
                v = prop[part, at // PER, at % PER]
                moved = v
                for b in range(7):
                    moved = jnp.where(jumps == b, pltpu.roll(v, 128 - (1 << b), 1), moved)
                for b in range(3):
                    moved = jnp.where(jumps == 7 + b, pltpu.roll(v, 8 - (1 << b), 0), moved)
                out_ref[part, chunk * PER + t] = moved * vacant
        return carry

    lax.fori_loop(0, CHUNKS, jump, 0)

    for number in range(KRYLOV + 1):
        pltpu.make_async_copy(gather.at[number], gather.at[number], red_send.at[number]).wait()
    for kind in range(4):
        for step in range(KRYLOV):
            pltpu.make_async_copy(big.at[OWN, step], big.at[OWN, step], send_sem.at[kind, step]).wait()


def body(amplitudes, couplings, fields, decays, channel):
    shape = (2, TILES, 8, 128)
    vmem = pl.BlockSpec(memory_space=pltpu.VMEM)
    smem = pl.BlockSpec(memory_space=pltpu.SMEM)
    chunk = (2, PER, 8, 128)
    out = pl.pallas_call(
        kernel,
        out_shape=jax.ShapeDtypeStruct(shape, f32),
        in_specs=[vmem, smem, smem, smem, smem],
        out_specs=vmem,
        scratch_shapes=[
            pltpu.VMEM((5, KRYLOV, CHUNKS, *chunk), f32),
            pltpu.VMEM((KRYLOV, CHUNKS, *chunk), f32),
            pltpu.VMEM((KRYLOV, CHUNKS, *chunk), f32),
            pltpu.VMEM((CHUNKS, *chunk), f32),
            pltpu.VMEM((CHUNKS, PER, 8, 128), f32),
            pltpu.VMEM((CHUNKS, PER, 8, 128), f32),
            pltpu.VMEM((CHUNKS, PER, 8, 128), f32),
            pltpu.VMEM((128, 128), f32),
            pltpu.VMEM((40, 8, 128), f32),
            pltpu.VMEM((KRYLOV + 1, 1, 128), f32),
            pltpu.VMEM((KRYLOV + 1, 15, 1, 128), f32),
            pltpu.VMEM((2, CHUNKS, PER, 8, 128), f32),
            pltpu.SemaphoreType.DMA((4, KRYLOV, CHUNKS)),
            pltpu.SemaphoreType.DMA((4, KRYLOV)),
            pltpu.SemaphoreType.DMA((KRYLOV + 1,)),
            pltpu.SemaphoreType.DMA((KRYLOV + 1,)),
        ],
        compiler_params=pltpu.CompilerParams(collective_id=0, has_side_effects=True),
    )(amplitudes.reshape(shape), couplings, fields, decays, channel)
    return out.reshape(amplitudes.shape)


def solution(mesh):
    placed = (P("traj", None, "amp"), P(), P(), P(), P("traj"))
    return jax.shard_map(
        body, mesh=mesh, in_specs=placed, out_specs=P("traj", None, "amp"), check_vma=False
    )
```

time: 855 us -> 94.8 us (0.11); the launches traced: 840 us -> 94.7 us
  other arithmetic: 366 us -> 0 us
  local copies, waits for them, and re-layouts: 155 us -> 3.49 us
  matrix products: 130 us -> 0 us
  starting transfers between devices: 105 us -> 0 us
  Pallas kernels: 0 us -> 90.5 us
  waiting for transfers between devices: 58.4 us -> 0 us
  between operations: 25.7 us -> 0.66 us
    dot_general x61 -> x0, matrix products: 130 us -> none  [the longest x8 47.3 us: body(): jnp.einsum('tcrl,lm->tcrm', apply_vector, lane_table, precision=highest)]
    sub x72 -> x0, other arithmetic: 105 us -> none  [the longest x8 98.2 us: body(): out_imag = diag_real * imag_part + diag_imag * real_part - flipped[:, 1]]
    neg x9 -> x0, other arithmetic: 98.7 us -> none  [the longest x8 98.7 us: body(): swapped = jnp.stack([applied[:, 1], -applied[:, 0]], axis=1)]
    pallas_call x0 -> x1, Pallas kernels: none -> 90.5 us  [body(): pl.pallas_call(kernel, out_shape=jax.ShapeDtypeStruct(shape, f32), in_spe...]
    mul x66 -> x0, other arithmetic: 81.5 us -> none  [the longest x64 81.5 us: body(): fields[apply_spin_pos] * flip_axis(apply_vector, 2, apply_spin_pos - 7)]
    all_to_all x12 -> x0, starting transfers between devices: 64.7 us -> none  [the longest x10 56.6 us: copy_for_each(): return lax.all_to_all(copies, axis, split_axis=0, concat_axis=0, tiled=True)]
    all_to_all x12 -> x0, waiting for transfers between devices: 53 us -> none  [the longest x10 37.8 us: copy_for_each(): return lax.all_to_all(copies, axis, split_axis=0, concat_axis=0, tiled=True)]
    another operation x39 -> x0, local copies, waits for them, and re-layouts: 44.4 us -> none
  transfers between devices with their start and end apart: 44 -> 0, of which waited for: 13 -> 0; matrix products, arithmetic and copies ran while one was open for 25% -> 0% of each run, Pallas kernels for 0% -> 0%
where the time goes in v1:
time: 94.8 us; the launch traced here: 94.7 us
  Pallas kernels  90.5 us (95%)
  local copies, waits for them, and re-layouts  3.49 us (4%)
    pallas_call x1, Pallas kernels, body(): pl.pallas_call(kernel, out_shape=jax.ShapeDtypeStruct(shape, f32), in_spe...  90.5 us

profile of v1, /device:TPU:128, one launch (start us, length us, event | category | flops | bytes accessed | tf_op | source)
XLA Modules:
  0.0 94.7 jit_solution(5059356027385293061)
XLA Ops:
  0.7 1.7 %copy.8 = f32[1,2,256,128]{3,2,1,0:T(8,128)} copy(f32[1,2,256,128]{3,1,2,0:T(2,128)} %bitcast.9) | data formatting | bytes 524288
  2.3 90.5 %shard_map.55 = f32[2,32,8,128]{3,2,1,0:T(8,128)} custom-call(f32[2,32,8,128]{3,2,1,0:T(8,128)} %bitcast.8, f32[18]{0:T(128)} %coup.1, f32[19]{0:T(128)} %field.1, f32[19]{0:T(128)} %decay.1, s32[1]{0:T(128)S(6)} %copy.9.chan), custom_call_target="tpu_custom_call" | custom-call | tf_op jit(solution)/shard_map/pallas_call | solution.py:397
  92.9 1.8 %reshape.7 = f32[1,2,32768]{2,1,0:T(2,128)} reshape(f32[2,32,8,128]{3,2,1,0:T(8,128)} %shard_map.55) | data formatting | bytes 524288 | tf_op jit(solution)/shard_map/reshape | solution.py:422

commit v2 on v1

v2 whole, which is shorter than its diff:
```python
import functools

import jax
import jax.numpy as jnp
from jax import lax
from jax.experimental import pallas as pl
from jax.experimental.pallas import tpu as pltpu
from jax.sharding import PartitionSpec as P

SPINS = 19
KRYLOV = 8
TILES = 32
CHUNKS = 16
PER = TILES // CHUNKS
CHUNK_BITS = CHUNKS.bit_length() - 1
LEAD = 8
TOTAL = KRYLOV * CHUNKS
TIME_STEP = 0.7
MESH = pl.DeviceIdType.MESH
OWN, DIR_Y, DIR_X, REL_Y, REL_X = range(5)
highest = lax.Precision.HIGHEST
f32 = jnp.float32


def flip(index, bit):
    step = 1 << bit
    return index + step - 2 * step * ((index // step) % 2)


def flip_by(index, mask):
    for bit in range(4):
        if mask >> bit & 1:
            index = flip(index, bit)
    return index


def wide(value):
    return jnp.broadcast_to(value, (8, 128))


def cmul(ar, ai, br, bi):
    return ar * br - ai * bi, ar * bi + ai * br


class Algebra:
    def __init__(self, sqrt, maximum, minimum):
        self.sqrt, self.maximum, self.minimum = sqrt, maximum, minimum
        self.r, self.ri, self.h, self.t, self.s, self.si = [], [], [], [], [], []

    @staticmethod
    def mul(a, b):
        if a[1] is None and b[1] is None:
            return a[0] * b[0], None
        if a[1] is None:
            return a[0] * b[0], a[0] * b[1]
        if b[1] is None:
            return a[0] * b[0], a[1] * b[0]
        return a[0] * b[0] - a[1] * b[1], a[0] * b[1] + a[1] * b[0]

    @staticmethod
    def join(a, b, sign):
        real = a[0] + b[0] if sign > 0 else a[0] - b[0]
        if b[1] is None:
            return real, a[1]
        if a[1] is None:
            return real, b[1] if sign > 0 else -b[1]
        return real, a[1] + b[1] if sign > 0 else a[1] - b[1]

    def dot(self, pairs, start=None, sign=1):
        total = start
        for a, b in pairs:
            term = self.mul(a, b)
            if total is None:
                total = term if sign > 0 else (-term[0], None if term[1] is None else -term[1])
            else:
                total = self.join(total, term, sign)
        return total

    def absorb(self, m, products, square, last=False):
        conj = lambda a: (a[0], None if a[1] is None else -a[1])
        r = [self.dot([(conj(self.ri[k][l]), products[l]) for l in range(k + 1)]) for k in range(m)]
        if not last:
            used = square
            for a in r:
                used = used - (a[0] * a[0] + a[1] * a[1])
            norm = self.sqrt(self.maximum(used, 1e-10 * square))
            inv = (1.0 / norm, None)
            ri = [self.mul(self.dot([(self.ri[k][l], r[k]) for k in range(l, m)], sign=-1), inv) for l in range(m)]
            self.ri.append(ri + [inv])
            self.r.append(r + [(norm, None)])
        else:
            self.r.append(r)
        if m > 0:
            c = m - 1
            col = self.t[c] + [(self.si[c], None)]
            rows = m if last else m + 1
            out = []
            for l in range(rows):
                a = self.dot([(col[k], self.r[k][l]) for k in range(l, m + 1)])
                a = self.dot([(self.r[c][k], self.h[k][l]) for k in range(max(l - 1, 0), c)], a, -1)
                out.append(self.mul(a, self.ri[c][c]))
            self.h.append(out)

    def start(self, shift, spread):
        root = self.sqrt(spread)
        s0 = 1.0 / root
        self.t.append([shift])
        self.s.append(s0)
        self.si.append(root)
        self.t.append([(spread * s0, None), shift])
        self.s.append(s0 * 0.70710678)
        self.si.append(root * 1.41421356)

    def predict(self, j):
        m = j - 1
        last = self.h[m - 1][m][0]
        last2 = last * last
        if m >= 2:
            before = self.h[m - 2][m - 1][0]
            rise = self.maximum(-0.5 * last2, self.minimum(last2, last2 - before * before))
            next2 = last2 + rise
        else:
            next2 = last2 * 1.5
        nxt = self.sqrt(next2)
        after = self.sqrt(self.maximum(2.0 * next2 - last2, 0.5 * next2))
        shift = self.h[m - 1][m - 1]
        guess = {m - 1: (last, None), m: shift}
        rows = []
        for l in range(m + 1):
            a = self.dot([(self.r[m][k], self.h[k][l]) for k in range(max(l - 1, 0), m)])
            if l in guess:
                a = self.dot([(self.r[m][m], guess[l])], a)
            a = self.dot([(self.t[m][k], self.r[k][l]) for k in range(l, m + 1)], a, -1)
            rows.append(self.mul(a, (self.s[m], None)))
        top = self.mul(self.r[m][m], (nxt * self.s[m], None))
        image = []
        for l in range(m + 1):
            a = self.dot([(rows[k], self.h[k][l]) for k in range(max(l - 1, 0), m)])
            if l in guess:
                a = self.dot([(rows[m], guess[l])], a)
            if l == m:
                a = self.dot([(top, (nxt, None))], a)
            image.append(a)
        lead = self.dot([(rows[m], (nxt, None)), (top, shift)])
        lead = self.mul(lead, (1.0 / top[0], None))
        rest = [self.join(image[l], self.mul(lead, rows[l]), -1) for l in range(m + 1)]
        t = [self.dot([(self.ri[k][l], rest[k]) for k in range(l, m + 1)]) for l in range(m + 1)]
        self.t.append(t + [lead])
        self.s.append(1.0 / after)
        self.si.append(after)


def matmul8(ar, ai, br, bi):
    out_r, out_i = None, None
    for k in range(KRYLOV):
        cr, ci = ar[:, k : k + 1], ai[:, k : k + 1]
        rr, ri = br[k : k + 1, :], bi[k : k + 1, :]
        tr, ti = cr * rr - ci * ri, cr * ri + ci * rr
        out_r = tr if out_r is None else out_r + tr
        out_i = ti if out_i is None else out_i + ti
    return out_r, out_i


def kernel(
    amp_ref, coup, field, decay, chan, out_ref,
    big, hbuf, diag_r, diag_i, mask_ref, lanes_ref, acc, total_ref, gather, prop,
    recv_sem, send_sem, red_recv, red_send,
):
    me = lax.axis_index("amp")
    y, x = me % 4, me // 4
    near_y, near_x = x * 4 + flip(y, 0), flip(x, 0) * 4 + y
    far_y, far_x = x * 4 + 3 - y, (3 - x) * 4 + y

    barrier = pltpu.get_barrier_semaphore()
    for mask in range(1, 16):
        pl.semaphore_signal(barrier, inc=1, device_id={"amp": flip_by(me, mask)}, device_id_type=MESH)

    lane = lax.broadcasted_iota(jnp.int32, (8, 128), 1)
    sub = lax.broadcasted_iota(jnp.int32, (8, 128), 0)
    low = sub * 128 + lane

    def copies(table, at):
        return [
            pltpu.make_async_remote_copy(
                src_ref=big.at[source, at], dst_ref=big.at[kind, at],
                send_sem=send_sem.at[kind - 1], recv_sem=recv_sem.at[kind - 1, at],
                device_id={"amp": target}, device_id_type=MESH)
            for kind, source, target in table
        ]

    def direct(at):
        return copies(((DIR_Y, OWN, near_y), (DIR_X, OWN, near_x)), at)

    def relay(at):
        return copies(((REL_Y, DIR_Y, far_y), (REL_X, DIR_X, far_x)), at)

    def sum_copy(number, mask):
        return pltpu.make_async_remote_copy(
            src_ref=total_ref.at[number], dst_ref=gather.at[number, mask - 1],
            send_sem=red_send.at[number], recv_sem=red_recv.at[number],
            device_id={"amp": flip_by(me, mask)}, device_id_type=MESH)

    def post_sums(number):
        rows = lax.broadcasted_iota(jnp.int32, (40, 128), 0)
        cols = lax.broadcasted_iota(jnp.int32, (40, 128), 1)
        by_lane = jnp.sum(acc[...], axis=1)
        by_row = jnp.sum(by_lane, axis=1, keepdims=True)
        total_ref[number] = jnp.sum(jnp.where(rows == cols, by_row, 0.0), axis=0, keepdims=True)
        for mask in range(1, 16):
            sum_copy(number, mask).start()

    def take_sums(number):
        pltpu.make_async_copy(gather.at[number], gather.at[number], red_recv.at[number]).wait()
        terms = [total_ref[number]] + [gather[number, i] for i in range(15)]
        while len(terms) > 1:
            terms = [terms[i] + terms[i + 1] for i in range(0, len(terms), 2)]
        return wide(terms[0])

    def pick(row, at):
        return wide(jnp.sum(jnp.where(lane == at, row, 0.0), axis=1, keepdims=True))

    def forward(at):
        for copy in direct(at):
            copy.wait_recv()
        for copy in relay(at):
            copy.start()

    for tile in range(TILES):
        for part in range(2):
            big[OWN, tile // PER, part, tile % PER] = amp_ref[tile * 8 : tile * 8 + 8, part]
    pl.semaphore_wait(barrier, 15)

    def send_first(at, carry):
        for copy in direct(at):
            copy.start()
        return carry

    lax.fori_loop(0, CHUNKS, send_first, 0)

    z = [1.0 - 2.0 * (low >> i & 1).astype(f32) for i in range(10)]
    base_r = jnp.zeros((8, 128), f32)
    base_i = jnp.zeros((8, 128), f32)
    for i in range(9):
        base_r = base_r - coup[i] * (z[i] * z[i + 1])
    for i in range(10):
        base_i = base_i - (0.25 * decay[i]) * (1.0 - z[i])
    zdev = [(1 - 2 * ((me // (1 << b)) % 2)).astype(f32) for b in range(4)]
    dev_r = -(coup[15] * zdev[0] * zdev[1] + coup[16] * zdev[1] * zdev[2] + coup[17] * zdev[2] * zdev[3])
    dev_i = jnp.float32(0.0)
    for b in range(4):
        dev_i = dev_i - 0.25 * decay[15 + b] * (1.0 - zdev[b])
    bond = coup[9] * z[9]
    channel = chan[0]
    shifts = jnp.full((8, 128), channel, jnp.int32)
    for tile in range(TILES):
        zt = [1.0 - 2.0 * (tile >> b & 1) for b in range(5)]
        sr, si = dev_r - coup[14] * zdev[0] * zt[4], dev_i
        for b in range(4):
            sr = sr - coup[10 + b] * (zt[b] * zt[b + 1])
        for b in range(5):
            if tile >> b & 1:
                si = si - 0.5 * decay[10 + b]
        diag_r[tile // PER, tile % PER] = (base_r - bond * zt[0]) + sr
        diag_i[tile // PER, tile % PER] = base_i + si
        spot = low + (tile * 1024 + me * 32768)
        mask_ref[tile // PER, tile % PER] = (spot >> shifts & 1).astype(f32)
    li = lax.broadcasted_iota(jnp.int32, (128, 128), 0)
    lj = lax.broadcasted_iota(jnp.int32, (128, 128), 1)
    table = jnp.zeros((128, 128), f32)
    for i in range(7):
        table = table + jnp.where((li ^ lj) == 1 << i, field[i], 0.0)
    lanes_ref[...] = table
    acc[...] = jnp.zeros((40, 8, 128), f32)

    def local_part(step, chunk):
        base = step * CHUNKS
        v = big[OWN, base + chunk]
        flips = lax.dot_general(
            v.reshape(2 * PER * 8, 128), lanes_ref[...], (((1,), (0,)), ((), ())),
            precision=highest, preferred_element_type=f32).reshape(2 * PER, 8, 128)
        w = v.reshape(2 * PER, 8, 128)
        s3 = lax.broadcasted_iota(jnp.int32, (2 * PER, 8, 128), 1)
        for b in range(2):
            rows = 1 << b
            up = pltpu.roll(w, 8 - rows, 1)
            down = pltpu.roll(w, rows, 1)
            flips = flips + field[7 + b] * jnp.where((s3 >> b & 1) == 0, up, down)
        flips = flips + field[9] * pltpu.roll(w, 4, 1)
        flips = flips.reshape(2, PER, 8, 128)
        for b in range(5 - CHUNK_BITS):
            order = [t ^ (1 << b) for t in range(PER)]
            flips = flips + field[10 + b] * jnp.concatenate([v[:, t : t + 1] for t in order], axis=1)
        for b in range(CHUNK_BITS):
            flips = flips + field[15 - CHUNK_BITS + b] * big[OWN, base + flip(chunk, b)]
        dr, di = diag_r[chunk], diag_i[chunk]
        hr = dr * v[0] - di * v[1] - flips[0]
        hi = dr * v[1] + di * v[0] - flips[1]
        return v, hr, hi

    def first(chunk, carry):
        v, hr, hi = local_part(0, chunk)
        hbuf[chunk, 0] = hr
        hbuf[chunk, 1] = hi
        acc[0] += jnp.sum(v[0] * hr + v[1] * hi, axis=0)
        acc[8] += jnp.sum(v[0] * hi - v[1] * hr, axis=0)
        acc[16] += jnp.sum(hr * hr + hi * hi, axis=0)
        acc[32] += jnp.sum(v[0] * v[0] + v[1] * v[1], axis=0)
        return carry

    lax.fori_loop(0, CHUNKS, first, 0)
    post_sums(0)

    def lead_in(at, carry):
        forward(at)
        return carry

    lax.fori_loop(0, LEAD, lead_in, 0)

    algebra = Algebra(jnp.sqrt, jnp.maximum, jnp.minimum)
    row = take_sums(0)
    square = pick(row, 32)
    algebra.absorb(0, [], square)
    beta = jnp.sqrt(square)
    shift = (pick(row, 0) / square, pick(row, 8) / square)
    spread = pick(row, 16) / square - (shift[0] * shift[0] + shift[1] * shift[1])
    for b in range(15, 19):
        spread = spread + field[b] * field[b]
    algebra.start(shift, spread)

    zero = jnp.zeros((8, 128), f32)
    proj_r, proj_i = zero, zero
    hess_r, hess_i = zero, zero

    def absorb(number):
        nonlocal proj_r, proj_i, hess_r, hess_i
        row = take_sums(number)
        products = [(pick(row, k), pick(row, 8 + k)) for k in range(min(number, KRYLOV))]
        algebra.absorb(number, products, pick(row, 32), last=number == KRYLOV)
        here = (sub == number - 1) & (lane < number)
        proj_r = jnp.where(here, pltpu.roll(row, 128 - 16, 1), proj_r)
        proj_i = jnp.where(here, pltpu.roll(row, 128 - 24, 1), proj_i)
        for l, value in enumerate(algebra.h[number - 1]):
            spot = (sub == number - 1) & (lane == l)
            hess_r = jnp.where(spot, value[0], hess_r)
            if value[1] is not None:
                hess_i = jnp.where(spot, value[1], hess_i)

    for step in range(KRYLOV):
        if step >= 2:
            absorb(step - 1)
            algebra.predict(step)
        ts, scale = algebra.t[step], algebra.s[step]
        acc[...] = jnp.zeros((40, 8, 128), f32)

        def advance(chunk, carry, step=step, ts=ts, scale=scale):
            at = step * CHUNKS + chunk
            if step + 1 < KRYLOV:
                forward(at + LEAD)
            else:
                @pl.when(chunk < CHUNKS - LEAD)
                def _():
                    forward(at + LEAD)
            if step == 0:
                h = hbuf[chunk]
            else:
                _, hr, hi = local_part(step, chunk)
                h = jnp.stack([hr, hi])
            h = h - (field[15] * big[DIR_Y, at] + field[17] * big[DIR_X, at])
            ur, ui = h[0], h[1]
            for k, t in enumerate(ts):
                p = big[OWN, k * CHUNKS + chunk]
                if t[1] is None:
                    ur, ui = ur - t[0] * p[0], ui - t[0] * p[1]
                else:
                    tr, ti = cmul(t[0], t[1], p[0], p[1])
                    ur, ui = ur - tr, ui - ti
            for copy in relay(at):
                copy.wait_recv()
            h = field[16] * big[REL_Y, at] + field[18] * big[REL_X, at]
            ur, ui = (ur - h[0]) * scale, (ui - h[1]) * scale
            if step + 1 < KRYLOV:
                big[OWN, at + CHUNKS, 0] = ur
                big[OWN, at + CHUNKS, 1] = ui
            m = mask_ref[chunk]
            v = big[OWN, at]
            mr, mi = m * v[0], m * v[1]
            for k in range(step + 1):
                p = big[OWN, k * CHUNKS + chunk]
                pr, pi = p[0], p[1]
                acc[k] += jnp.sum(pr * ur + pi * ui, axis=0)
                acc[8 + k] += jnp.sum(pr * ui - pi * ur, axis=0)
                acc[16 + k] += jnp.sum(pr * mr + pi * mi, axis=0)
                acc[24 + k] += jnp.sum(pr * mi - pi * mr, axis=0)
            acc[32] += jnp.sum(ur * ur + ui * ui, axis=0)
            if step + 1 < KRYLOV:
                for copy in direct(at + CHUNKS):
                    copy.start()
            return carry

        lax.fori_loop(0, CHUNKS, advance, 0)
        post_sums(step + 1)

    absorb(KRYLOV - 1)
    absorb(KRYLOV)

    size = TIME_STEP / 256.0
    ar, ai = size * hess_i, -size * hess_r
    eye = jnp.where(sub == lane, 1.0, 0.0)
    er, ei = eye, zero
    for degree in range(10, 0, -1):
        tr, ti = matmul8(ar, ai, er, ei)
        er, ei = eye + tr * (1.0 / degree), ti * (1.0 / degree)
    for _ in range(8):
        er, ei = matmul8(er, ei, er, ei)
    first_r, first_i = wide(er[:1]) * beta, wide(ei[:1]) * beta
    weights = [(pick(first_r, k), pick(first_i, k)) for k in range(KRYLOV)]
    ds = [algebra.dot([(algebra.ri[k][l], weights[k]) for k in range(l, KRYLOV)]) for l in range(KRYLOV)]
    across_r, across_i, along_r, along_i = zero, zero, zero, zero
    for k, (dr, di) in enumerate(ds):
        across_r, across_i = jnp.where(lane == k, dr, across_r), jnp.where(lane == k, di, across_i)
        along_r, along_i = jnp.where(sub == k, dr, along_r), jnp.where(sub == k, di, along_i)
    pair_r, pair_i = cmul(across_r, -across_i, along_r, along_i)
    weighed = jnp.where(lane < sub, 2.0, 1.0) * (pair_r * proj_r - pair_i * proj_i)
    held = wide(jnp.sum(jnp.sum(weighed, axis=1, keepdims=True), axis=0, keepdims=True))
    held = jnp.where(shifts < SPINS, held, 524288.0)
    factor = jnp.sqrt(524288.0 / held)
    ds = [(dr * factor, di * factor) for dr, di in ds]

    source = jnp.where(channel == 15, DIR_Y, OWN)
    source = jnp.where(channel == 17, DIR_X, source)
    source = jnp.where(channel == 16, REL_Y, source)
    source = jnp.where(channel == 18, REL_X, source)

    def combine(chunk, carry):
        tot_r, tot_i = None, None
        for k, (dr, di) in enumerate(ds):
            v = big[source, k * CHUNKS + chunk]
            tr, ti = cmul(dr, di, v[0], v[1])
            tot_r = tr if tot_r is None else tot_r + tr
            tot_i = ti if tot_i is None else tot_i + ti
        prop[0, chunk] = tot_r
        prop[1, chunk] = tot_i
        return carry

    lax.fori_loop(0, CHUNKS, combine, 0)
    delta = jnp.where((channel >= 10) & (channel < 15), jnp.left_shift(1, jnp.clip(channel - 10, 0, 4)), 0)

    def jump(chunk, carry):
        for t in range(PER):
            at = jnp.minimum(chunk * PER + t + delta, TILES - 1)
            vacant = 1.0 - mask_ref[chunk, t]
            for part in range(2):
                v = prop[part, at // PER, at % PER]
                moved = v
                for b in range(7):
                    moved = jnp.where(shifts == b, pltpu.roll(v, 128 - (1 << b), 1), moved)
                for b in range(3):
                    moved = jnp.where(shifts == 7 + b, pltpu.roll(v, 8 - (1 << b), 0), moved)
                out_ref[pl.ds((chunk * PER + t) * 8, 8), part] = moved * vacant
        return carry

    lax.fori_loop(0, CHUNKS, jump, 0)

    for number in range(KRYLOV + 1):
        pltpu.make_async_copy(gather.at[number], gather.at[number], red_send.at[number]).wait()
    for kind in range(4):
        pltpu.make_async_copy(big.at[OWN], big.at[OWN], send_sem.at[kind]).wait()


def body(amplitudes, couplings, fields, decays, channel):
    vmem = pl.BlockSpec(memory_space=pltpu.VMEM)
    smem = pl.BlockSpec(memory_space=pltpu.SMEM)
    chunk = (2, PER, 8, 128)
    out = pl.pallas_call(
        kernel,
        out_shape=jax.ShapeDtypeStruct((TILES * 8, 2, 128), f32),
        in_specs=[vmem, smem, smem, smem, smem],
        out_specs=vmem,
        scratch_shapes=[
            pltpu.VMEM((5, TOTAL, *chunk), f32),
            pltpu.VMEM((CHUNKS, *chunk), f32),
            pltpu.VMEM((CHUNKS, PER, 8, 128), f32),
            pltpu.VMEM((CHUNKS, PER, 8, 128), f32),
            pltpu.VMEM((CHUNKS, PER, 8, 128), f32),
            pltpu.VMEM((128, 128), f32),
            pltpu.VMEM((40, 8, 128), f32),
            pltpu.VMEM((KRYLOV + 1, 1, 128), f32),
            pltpu.VMEM((KRYLOV + 1, 15, 1, 128), f32),
            pltpu.VMEM((2, CHUNKS, PER, 8, 128), f32),
            pltpu.SemaphoreType.DMA((4, TOTAL)),
            pltpu.SemaphoreType.DMA((4,)),
            pltpu.SemaphoreType.DMA((KRYLOV + 1,)),
            pltpu.SemaphoreType.DMA((KRYLOV + 1,)),
        ],
        compiler_params=pltpu.CompilerParams(collective_id=0, has_side_effects=True),
    )(amplitudes.reshape(2, TILES * 8, 128).transpose(1, 0, 2), couplings, fields, decays, channel)
    return out.transpose(1, 0, 2).reshape(amplitudes.shape)


def solution(mesh):
    placed = (P("traj", None, "amp"), P(), P(), P(), P("traj"))
    return jax.shard_map(
        body, mesh=mesh, in_specs=placed, out_specs=P("traj", None, "amp"), check_vma=False
    )
```

time: 94.8 us -> 82.8 us (0.87)
  Pallas kernels: 90.5 us -> 80.3 us
  local copies, waits for them, and re-layouts: 3.49 us -> 1.67 us
    pallas_call x1, Pallas kernels: 90.5 us -> 80.3 us  [body(): pl.pallas_call(kernel, out_shape=jax.ShapeDtypeStruct((TILES * 8, 2, 128)...]
    reshape x1 -> x0, local copies, waits for them, and re-layouts: 1.82 us -> none  [body(): return out.reshape(amplitudes.shape)]
where the time goes in v2:
time: 82.8 us; the launch traced here: 82.6 us
  Pallas kernels  80.3 us (97%)
  local copies, waits for them, and re-layouts  1.67 us (2%)
    pallas_call x1, Pallas kernels, body(): pl.pallas_call(kernel, out_shape=jax.ShapeDtypeStruct((TILES * 8, 2, 128)...  80.3 us
    unnamed x1, local copies, waits for them, and re-layouts  1.67 us

profile of v2, /device:TPU:128, one launch (start us, length us, event | category | flops | bytes accessed | tf_op | source)
XLA Modules:
  0.0 82.6 jit_solution(9394087082990010622)
XLA Ops:
  0.7 80.3 %shard_map.55 = f32[256,2,128]{2,1,0:T(2,128)} custom-call(f32[256,2,128]{2,1,0:T(2,128)} %bitcast.7, f32[18]{0:T(128)} %coup.1, f32[19]{0:T(128)} %field.1, f32[19]{0:T(128)} %decay.1, s32[1]{0:T(128)S(6)} %copy.7.chan), custom_call_target="tpu_custom_call" | custom-call | tf_op jit(solution)/shard_map/pallas_call | solution.py:474
  81.0 1.7 %copy.8 = f32[1,2,32768]{2,1,0:T(2,128)} copy(f32[1,2,32768]{2,1,0:T(2,128)} %bitcast.6) | data formatting | bytes 524288
